TPU v7x, 256 devices: a whole 4x4x8 slice. The times are simulated.
256 devices in a mesh: layer: 4 (over z_lo, core), harm: 64 (over y, z_hi, x).
Axes of the slice: x: 4, y: 4, z: 8 (z_hi: 4, z_lo: 2; z = z_hi * 2 + z_lo), core: 2. Of those that a mesh axis runs over, the one named last changes fastest.
Arguments:
- source: bfloat16 [2, 2048, 128], P(None, 'harm'), may hold values from -6 to 6
- transfer: bfloat16 [4, 2, 2048, 2048], P('layer', None, 'harm'), may hold values from -0.09375 to 0.09375
- fields: bfloat16 [4, 2, 2048, 128], P('layer', None, 'harm'), may hold values from -6 to 6
- orders: int32 [2048], replicated, may hold values from 0 to 2047, each once
Outputs:
- gradients: float32 [4, 2, 4096], P('layer', None, 'harm')
- boundary: bfloat16 [4, 2, 2048, 128], P('layer', None, 'harm')
Inputs may be any that keep to these rules, and one draw needn't show every extreme that they name: `orders`: every value from 0 to 2047 appears exactly once.
All inputs are finite; a program needn't handle non-finite values.
Results may differ from a plain program's by a relative error of at most 0.006.
Values may be sent and summed in bfloat16 or wider, within the bound.
A program may use at most 64 MiB of HBM per device.

v0:
```python
import math
import jax
import jax.numpy as jnp
from jax import lax
from jax.sharding import PartitionSpec as P


def in_order(blocks, dim):
    blocks = jnp.moveaxis(blocks, 0, dim)
    dims = blocks.shape
    return blocks.reshape(*dims[:dim], dims[dim] * dims[dim + 1], *dims[dim + 2 :])


def from_everyone(value, axis):
    copies = jnp.broadcast_to(value, (lax.axis_size(axis), *value.shape))
    return lax.all_to_all(copies, axis, split_axis=0, concat_axis=0, tiled=True)


def gather_directly(value, axis, dim):
    return in_order(from_everyone(value, axis), dim)


def shifted(value, axis, steps):
    count = lax.axis_size(axis)
    first, last = (max(0, -steps), min(count, count - steps))
    return lax.ppermute(value, axis, [(source, source + steps) for source in range(first, last)])


def correlate(adjoint, forward, position, band_start, band_width):
    harmonics = adjoint.shape[1]
    columns = adjoint.shape[2]
    adj_sorted = jnp.take(adjoint, position, axis=1)
    fwd_sorted = jnp.take(forward, position, axis=1)
    padded = jnp.pad(adj_sorted, ((0, 0), (harmonics, harmonics + 1), (0, 0)))
    window_slab = lax.dynamic_slice_in_dim(padded, band_start + 1, harmonics + band_width, 1)
    count = harmonics // band_width
    blocks = window_slab.reshape(2, count + 1, band_width, columns)
    windows = jnp.concatenate([blocks[:, :-1], blocks[:, 1:]], axis=2)
    forward_blocks = fwd_sorted.reshape(2, count, band_width, columns)

    def product(left_part, right_part):
        return jnp.einsum("nkb,ncb->nkc", left_part, right_part, preferred_element_type=jnp.float32)

    real_part = product(forward_blocks[0], windows[0]) - product(forward_blocks[1], windows[1])
    imag_part = product(forward_blocks[0], windows[1]) + product(forward_blocks[1], windows[0])

    def diagonals(result_block):
        flattened = result_block.reshape(count, band_width * 2 * band_width)
        flattened = jnp.pad(flattened, ((0, 0), (0, band_width)))
        shaped = flattened.reshape(count, band_width, 2 * band_width + 1)[:, :, :band_width]
        return jnp.sum(shaped, axis=(0, 1))

    return jnp.stack([diagonals(real_part), diagonals(imag_part)])


def gather_rows(adjoint):
    return lax.all_gather(adjoint, "harm", axis=1, tiled=True)


def spread_fields(local_fields):
    return gather_directly(local_fields, "harm", 2)


def propagate(matrix, gathered):
    real_part = jnp.dot(matrix[0], gathered[0], preferred_element_type=jnp.float32) - jnp.dot(
        matrix[1], gathered[1], preferred_element_type=jnp.float32
    )
    imag_part = jnp.dot(matrix[0], gathered[1], preferred_element_type=jnp.float32) + jnp.dot(
        matrix[1], gathered[0], preferred_element_type=jnp.float32
    )
    return jnp.stack([real_part, imag_part]).astype(jnp.bfloat16)


def per_device(source, transfer, fields, orders):
    harmonics = orders.shape[0]
    sections = lax.axis_size("layer")
    section_index = lax.axis_index("layer")
    band_width = 2 * harmonics // lax.axis_size("harm")
    band_start = lax.axis_index("harm") * band_width
    rows_dev = transfer.shape[2]
    columns = source.shape[2]
    norm_scale = 1.0 / math.sqrt(harmonics * columns)
    position = (
        jnp.zeros((harmonics,), jnp.int32).at[orders].set(jnp.arange(harmonics, dtype=jnp.int32))
    )
    layers_here = transfer.shape[0]
    field_source = spread_fields(fields)
    micro_count = 1
    micro_cols = columns // micro_count
    stored = jnp.zeros((layers_here, 2, harmonics, columns), jnp.bfloat16)
    bottom = jnp.zeros((2, rows_dev, columns), jnp.bfloat16)
    incoming = jnp.zeros((2, rows_dev, micro_cols), jnp.bfloat16)
    total_steps = sections + micro_count - 1
    for step_index in range(total_steps):
        micro_index = step_index - (sections - 1 - section_index)
        active = (micro_index >= 0) & (micro_index < micro_count)
        if step_index < micro_count:
            top_source = source
        else:
            top_source = jnp.zeros_like(incoming)
        adjoint = jnp.where(section_index == sections - 1, top_source, incoming)
        gathered = gather_rows(adjoint)
        stored = stored.at[0].set(jnp.where(active, gathered, stored[0]))
        adjoint = propagate(transfer[0], gathered)
        bottom = jnp.where(active, adjoint, bottom)
        if step_index < total_steps - 1:
            incoming = shifted(adjoint, "layer", -1)
    grads = jnp.stack(
        [correlate(stored[0], field_source[0], position, band_start, band_width) * norm_scale]
    )
    return (grads, bottom[None])


def solution(mesh):
    return jax.shard_map(
        per_device,
        mesh=mesh,
        in_specs=(
            P(None, "harm", None),
            P("layer", None, "harm", None),
            P("layer", None, "harm", None),
            P(),
        ),
        out_specs=(P("layer", None, "harm"), P("layer", None, "harm", None)),
        check_vma=False,
    )
```

profile of v0, /device:TPU:8, one launch (start us, length us, event | category | flops | bytes accessed | tf_op | source)
XLA Modules:
  0.0 404.4 jit_solution(10969838108467156854)
XLA Ops:
  8.0 81.3 %all-gather.5.cloned.1.call-done = bf16[2,2048,128]{2,1,0:T(8,128)(2,1)} async-done(((bf16[2,32,128]{2,1,0:T(8,128)(2,1)}), bf16[2,2048,128]{2,1,0:T(8,128)(2,1)}) %all-gather.5.cloned.1.call-update) | async-done | bytes 1048592 | tf_op jit(solution)/shard_map/all_gather | solution.py:57
  89.2 1.4 fusion.15
  90.6 1.3 fusion.16
  92.0 1.3 fusion
  94.8 1.8 collective-permute-done
  97.3 72.2 %all-gather.7.cloned.1.call-done = bf16[2,2048,128]{2,1,0:T(8,128)(2,1)} async-done(((bf16[2,32,128]{2,1,0:T(8,128)(2,1)}), bf16[2,2048,128]{2,1,0:T(8,128)(2,1)}) %all-gather.7.cloned.1.call-update) | async-done | bytes 1048592 | tf_op jit(solution)/shard_map/all_gather | solution.py:57
  169.5 1.3 fusion.18
  174.9 1.8 collective-permute-done.1
  177.3 72.3 %all-gather.9.cloned.1.call-done = bf16[2,2048,128]{2,1,0:T(8,128)(2,1)} async-done(((bf16[2,32,128]{2,1,0:T(8,128)(2,1)}), bf16[2,2048,128]{2,1,0:T(8,128)(2,1)}) %all-gather.9.cloned.1.call-update) | async-done | bytes 1048592 | tf_op jit(solution)/shard_map/all_gather | solution.py:57
  249.6 1.3 fusion.20
  256.3 8.7 %all-to-all-start = ((bf16[64,1,2,32,128]{4,3,2,1,0:T(8,128)(2,1)}), bf16[64,1,2,32,128]{4,3,2,1,0:T(8,128)(2,1)S(1)}, u32[]{:S(2)}, u32[]{:S(2)}) async-start(bf16[64,1,2,32,128]{4,3,2,1,0:T(8,128)(2,1)} %broadcast_in_dim.17), calls=%async_computation | async-start | bytes 2097152 | tf_op jit(solution)/shard_map/all_to_all | solution.py:16
  265.7 8.2 %scatter_custom_fusion = s32[2048]{0:T(1024)S(1)} fusion(s32[2048]{0:T(1024)S(1)} %compare_select_fusion.1, s32[2048]{0:T(1024)S(1)} %iota.3, s32[]{:T(128)} %constant.110.clone.1), kind=kCustom, calls=%fused_computation.103 | custom fusion | bytes 8196 | tf_op jit(solution)/shard_map/scatter | solution.py:84
  274.0 21.0 %all-to-all-done = bf16[64,1,2,32,128]{4,3,2,1,0:T(8,128)(2,1)S(1)} async-done(((bf16[64,1,2,32,128]{4,3,2,1,0:T(8,128)(2,1)}), bf16[64,1,2,32,128]{4,3,2,1,0:T(8,128)(2,1)S(1)}, u32[]{:S(2)}, u32[]{:S(2)}) %all-to-all-start) | async-done | bytes 1048608 | tf_op jit(solution)/shard_map/all_to_all | solution.py:16
  295.1 8.7 %copy.13 = bf16[2,2048,128]{2,0,1:T(2,128)(2,1)S(1)} copy(bf16[2,2048,128]{2,1,0:T(8,128)(2,1)S(1)} %bitcast.145) | data formatting | bytes 2097152 | tf_op jit(solution)/shard_map/squeeze;reshape | solution.py:109
  303.8 7.1 %gather_fusion = bf16[2048,2,128]{2,1,0:T(2,128)(2,1)S(1)} fusion(bf16[2,2048,128]{2,0,1:T(2,128)(2,1)S(1)} %copy.13, s32[2048]{0:T(1024)S(1)} %fusion.58), kind=kCustom, calls=%fused_computation.clone | custom fusion | bytes 2105344 | tf_op jit(solution)/shard_map/jit(_take)/gather | solution.py:33
  310.8 36.5 %all-gather.11.cloned.1.call-done = bf16[2,2048,128]{2,1,0:T(8,128)(2,1)} async-done(((bf16[2,32,128]{2,1,0:T(8,128)(2,1)}), bf16[2,2048,128]{2,1,0:T(8,128)(2,1)}) %all-gather.11.cloned.1.call-update) | async-done | bytes 1048592 | tf_op jit(solution)/shard_map/all_gather | solution.py:57
  347.4 1.4 select_select_fusion
  348.8 8.7 %copy.14 = bf16[2,2048,128]{2,0,1:T(2,128)(2,1)S(1)} copy(bf16[2,2048,128]{2,1,0:T(8,128)(2,1)S(1)} %select_select_fusion) | data formatting | bytes 2097152 | tf_op jit(solution)/shard_map/jit(_where)/select_n | solution.py:103
  357.5 7.1 %gather_fusion.1 = bf16[2048,2,128]{2,1,0:T(2,128)(2,1)S(1)} fusion(bf16[2,2048,128]{2,0,1:T(2,128)(2,1)S(1)} %copy.14, s32[2048]{0:T(1024)S(1)} %fusion.58), kind=kCustom, calls=%fused_computation.1.clone | custom fusion | bytes 2105344 | tf_op jit(solution)/shard_map/jit(_take)/gather | solution.py:32
  364.5 7.6 %fusion.14 = (bf16[2,2048,128]{2,0,1:T(2,128)(2,1)S(1)}, bf16[2,2048,128]{2,0,1:T(2,128)(2,1)S(1)}) fusion(bf16[2048,2,128]{2,1,0:T(2,128)(2,1)S(1)} %gather_fusion.1, pred[2048]{0:T(1024)(128)(4,1)S(1)} %compare_and_fusion, bf16[2048,2,128]{2,1,0:T(2,128)(2,1)S(1)} %gather_fusion), kind=kLoop, calls=%fused_computation.38 | loop fusion | flops 1048576 | bytes 4196352 | tf_op jit(solution)/shard_map/jit(_take)/select_n | solution.py:32
  372.1 6.4 %pad_dynamic-slice_fusion = bf16[2,2112,128]{2,0,1:T(2,128)(2,1)S(1)} fusion(s32[]{:T(128)S(6)} %select_n.125, bf16[2,2048,128]{2,0,1:T(2,128)(2,1)S(1)} %get-tuple-element.55), kind=kLoop, calls=%fused_computation.3 | loop fusion | bytes 2129924 | tf_op jit(solution)/shard_map/dynamic_slice | solution.py:35
  379.3 1.5 fusion.67
  386.7 3.8 reshape.351
  390.7 2.7 reshape.353
  (66 shorter events, 24.8 us)
Async XLA Ops:
  7.2 86.1 %copy-start.6 = (bf16[1,2,32,2048]{3,2,1,0:T(8,128)(2,1)S(1)}, bf16[1,2,32,2048]{3,2,1,0:T(8,128)(2,1)}, u32[]{:S(2)}) copy-start(bf16[1,2,32,2048]{3,2,1,0:T(8,128)(2,1)} %param.15) | copy-start | bytes 786436
  7.2 82.1 %all-gather.5.cloned.1.call-start = ((), (), s32[]{:S(2)}) async-start(), calls=%async_computation.1 | async-start | bytes 1064960 | tf_op jit(solution)/shard_map/all_gather | solution.py:57
  7.9 161.6 %all-gather.7.cloned.1.call-start = ((), (), s32[]{:S(2)}) async-start(), calls=%async_computation.2 | async-start | bytes 1064960 | tf_op jit(solution)/shard_map/all_gather | solution.py:57
  89.2 4.1 %copy-start = (bf16[2,2048,128]{2,1,0:T(8,128)(2,1)S(1)}, bf16[2,2048,128]{2,1,0:T(8,128)(2,1)}, u32[]{:S(2)}) copy-start(bf16[2,2048,128]{2,1,0:T(8,128)(2,1)} %all-gather.5.cloned.1.call-done) | copy-start | bytes 3145732
  93.5 3.1 collective-permute-start
  97.2 152.4 %all-gather.9.cloned.1.call-start = ((), (), s32[]{:S(2)}) async-start(), calls=%async_computation.3 | async-start | bytes 1064960 | tf_op jit(solution)/shard_map/all_gather | solution.py:57
  169.5 3.9 copy-start.1
  172.1 82.9 %copy-start.4 = (bf16[1,2,32,128]{3,2,1,0:T(8,128)(2,1)S(1)}, bf16[1,2,32,128]{3,2,1,0:T(8,128)(2,1)}, u32[]{:S(2)}) copy-start(bf16[1,2,32,128]{3,2,1,0:T(8,128)(2,1)} %param.16) | copy-start | bytes 49156
  173.6 3.1 collective-permute-start.1
  249.6 3.8 copy-start.3
  253.5 12.2 %copy-start.5 = (s32[2048]{0:T(1024)S(1)}, s32[2048]{0:T(1024)}, u32[]{:S(2)}) copy-start(s32[2048]{0:T(1024)} %param.17) | copy-start | bytes 24580
  253.7 11.3 %collective-permute-start.2 = (bf16[2,32,128]{2,1,0:T(8,128)(2,1)S(1)}, bf16[2,32,128]{2,1,0:T(8,128)(2,1)S(1)}, u32[]{:S(2)}, u32[]{:S(2)}) collective-permute-start(bf16[2,32,128]{2,1,0:T(8,128)(2,1)S(1)} %pad_maximum_fusion.3), channel_id=1, source_target_pairs={{64,0},{128,64},{192,128},{65,1},{129,65},{193,129},{66,2},{130,66... | collective-permute-start | bytes 49160 | tf_op jit(solution)/shard_map/ppermute | solution.py:26
  256.3 38.7 %all-to-all-start = ((bf16[64,1,2,32,128]{4,3,2,1,0:T(8,128)(2,1)}), bf16[64,1,2,32,128]{4,3,2,1,0:T(8,128)(2,1)S(1)}, u32[]{:S(2)}, u32[]{:S(2)}) async-start(bf16[64,1,2,32,128]{4,3,2,1,0:T(8,128)(2,1)} %broadcast_in_dim.17), calls=%async_computation | async-start | bytes 2097152 | tf_op jit(solution)/shard_map/all_to_all | solution.py:16
  264.9 82.4 %all-gather.11.cloned.1.call-start = ((), (), s32[]{:S(2)}) async-start(), calls=%async_computation.4 | async-start | bytes 1064960 | tf_op jit(solution)/shard_map/all_gather | solution.py:57
  393.4 3.4 copy-start.2
Sparse Core Ops, SparseCore 0:
  11.7 77.4 all-gather.4
  97.4 72.1 all-gather.6
  177.4 72.1 all-gather.8
  269.2 78.1 all-gather.10
where the time goes:
time: 405 us; the launch traced here: 404 us
  waiting for transfers between devices  287 us (71%)
  local copies, waits for them, and re-layouts  58.7 us (14%)
  matrix products  18.4 us (5%)
  between operations  14.2 us (4%)
  other arithmetic  13.3 us (3%)
  starting transfers between devices  12.7 us (3%)
    all_gather x4, waiting for transfers between devices, gather_rows(): return lax.all_gather(adjoint, 'harm', axis=1, tiled=True)  262 us
    all_to_all x1, waiting for transfers between devices, from_everyone(): return lax.all_to_all(copies, axis, split_axis=0, concat_axis=0, tiled=True)  21 us
    all_to_all x1, starting transfers between devices, from_everyone(): return lax.all_to_all(copies, axis, split_axis=0, concat_axis=0, tiled=True)  8.68 us
    another operation x1, local copies, waits for them, and re-layouts, per_device(): field_source[0]  8.68 us
    select_n x1, local copies, waits for them, and re-layouts, per_device(): stored = stored.at[0].set(jnp.where(active, gathered, stored[0]))  8.68 us
    scatter x1, local copies, waits for them, and re-layouts, per_device(): jnp.zeros((harmonics,), jnp.int32).at[orders]  8.23 us
  transfers between devices with their start and end apart: 8, of which 7 were waited for; matrix products, arithmetic and copies ran while one was open for 6% of the time, Pallas kernels for 0%

commit v1 on v0

--- a/solution.py
+++ b/solution.py
@@ -3,6 +3,13 @@
 import jax.numpy as jnp
 from jax import lax
 from jax.sharding import PartitionSpec as P
+
+
+def swapped_in(x, mesh_axis, dim):
+    devices = lax.axis_size(mesh_axis)
+    blocks = jnp.stack([x for _ in range(devices)])
+    blocks = lax.all_to_all(blocks, mesh_axis, split_axis=0, concat_axis=0)
+    return jnp.concatenate(blocks, axis=dim)
 
 
 def in_order(blocks, dim):
@@ -54,7 +61,7 @@
 
 
 def gather_rows(adjoint):
-    return lax.all_gather(adjoint, "harm", axis=1, tiled=True)
+    return swapped_in(adjoint, "harm", 1)
 
 
 def spread_fields(local_fields):

time: 405 us -> 250 us (0.62)
  waiting for transfers between devices: 287 us -> 30 us
  blocking collectives: 0 us -> 114 us
  between operations: 14.2 us -> 1.14 us
  matrix products: 18.4 us -> 6.59 us
  starting transfers between devices: 12.7 us -> 21.5 us
  local copies, waits for them, and re-layouts: 58.7 us -> 65.3 us
    all_gather x4 -> x0, waiting for transfers between devices: 262 us -> none  [gather_rows(): return lax.all_gather(adjoint, 'harm', axis=1, tiled=True)]
    all_to_all x0 -> x3, blocking collectives: none -> 114 us  [swapped_in(): blocks = lax.all_to_all(blocks, mesh_axis, split_axis=0, concat_axis=0)]
    gather x1, local copies, waits for them, and re-layouts: 7.05 us -> 15 us  [correlate(): fwd_sorted = jnp.take(forward, position, axis=1)]
    all_to_all x0 -> x1, starting transfers between devices: none -> 7.91 us  [swapped_in(): blocks = lax.all_to_all(blocks, mesh_axis, split_axis=0, concat_axis=0)]
    select_n x1, local copies, waits for them, and re-layouts: 8.68 us -> 1.08 us  [per_device(): stored = stored.at[0].set(jnp.where(active, gathered, stored[0]))]
    dot_general x4, matrix products: 5.2 us -> 0.81 us  [propagate(): jnp.dot(matrix[1], gathered[1], preferred_element_type=jnp.float32)]
  transfers between devices with their start and end apart: 8 -> 5, of which waited for: 7 -> 4; matrix products, arithmetic and copies ran while one was open for 6% -> 14% of each run, Pallas kernels for 0% -> 0%
where the time goes in v1:
time: 250 us; the launch traced here: 249 us
  blocking collectives  114 us (46%)
  local copies, waits for them, and re-layouts  65.3 us (26%)
  waiting for transfers between devices  30 us (12%)
  starting transfers between devices  21.5 us (9%)
  other arithmetic  10.9 us (4%)
  matrix products  6.59 us (3%)
    all_to_all x3, blocking collectives, swapped_in(): blocks = lax.all_to_all(blocks, mesh_axis, split_axis=0, concat_axis=0)  114 us
    all_to_all x1, waiting for transfers between devices, from_everyone(): return lax.all_to_all(copies, axis, split_axis=0, concat_axis=0, tiled=True)  22.9 us
    gather x1, local copies, waits for them, and re-layouts, correlate(): fwd_sorted = jnp.take(forward, position, axis=1)  15 us
    all_to_all x1, starting transfers between devices, from_everyone(): return lax.all_to_all(copies, axis, split_axis=0, concat_axis=0, tiled=True)  9.76 us
    another operation x1, local copies, waits for them, and re-layouts, per_device(): field_source[0]  9.45 us
    scatter x1, local copies, waits for them, and re-layouts, per_device(): jnp.zeros((harmonics,), jnp.int32).at[orders]  8.23 us
    all_to_all x1, starting transfers between devices, swapped_in(): blocks = lax.all_to_all(blocks, mesh_axis, split_axis=0, concat_axis=0)  7.91 us
    select_n x1, other arithmetic, correlate(): adj_sorted = jnp.take(adjoint, position, axis=1)  7.59 us
  transfers between devices with their start and end apart: 5, of which 4 were waited for; matrix products, arithmetic and copies ran while one was open for 14% of the time, Pallas kernels for 0%

profile of v1, /device:TPU:8, one launch (start us, length us, event | category | flops | bytes accessed | tf_op | source)
XLA Modules:
  0.0 249.4 jit_solution(94307073561378878)
XLA Ops:
  0.9 38.9 %all_to_all.25 = bf16[64,2,32,128]{3,2,1,0:T(8,128)(2,1)S(1)} all-to-all(bf16[64,2,32,128]{3,2,1,0:T(8,128)(2,1)S(1)} %stack.65), channel_id=1, replica_groups=mesh['layer'=4,'harm'=64] {'harm'}, dimensions={0} | all-to-all | bytes 2097152 | tf_op jit(solution)/shard_map/all_to_all | solution.py:11
  41.6 1.3 collective-permute-start
  42.9 1.8 collective-permute-done
  44.9 36.7 %all_to_all.26 = bf16[64,2,32,128]{3,2,1,0:T(8,128)(2,1)S(1)} all-to-all(bf16[64,2,32,128]{3,2,1,0:T(8,128)(2,1)S(1)} %stack.69), channel_id=1, replica_groups=mesh['layer'=4,'harm'=64] {'harm'}, dimensions={0} | all-to-all | bytes 2097152 | tf_op jit(solution)/shard_map/all_to_all | solution.py:11
  82.7 1.3 collective-permute-start.1
  84.0 3.5 %collective-permute-done.1 = bf16[2,32,128]{2,1,0:T(8,128)(2,1)S(1)} collective-permute-done((bf16[2,32,128]{2,1,0:T(8,128)(2,1)S(1)}, bf16[2,32,128]{2,1,0:T(8,128)(2,1)S(1)}, u32[]{:S(2)}, u32[]{:S(2)}) %collective-permute-start.1) | collective-permute-done | bytes 16416 | tf_op jit(solution)/shard_map/ppermute | solution.py:33
  87.7 38.3 %all_to_all.27 = bf16[64,2,32,128]{3,2,1,0:T(8,128)(2,1)S(1)} all-to-all(bf16[64,2,32,128]{3,2,1,0:T(8,128)(2,1)S(1)} %stack.73), channel_id=1, replica_groups=mesh['layer'=4,'harm'=64] {'harm'}, dimensions={0} | all-to-all | bytes 2097152 | tf_op jit(solution)/shard_map/all_to_all | solution.py:11
  127.3 9.8 %all-to-all-start = ((bf16[64,1,2,32,128]{4,3,2,1,0:T(8,128)(2,1)}), bf16[64,1,2,32,128]{4,3,2,1,0:T(8,128)(2,1)}, u32[]{:S(2)}, u32[]{:S(2)}) async-start(bf16[64,1,2,32,128]{4,3,2,1,0:T(8,128)(2,1)} %broadcast_in_dim.17), calls=%async_computation | async-start | bytes 2097152 | tf_op jit(solution)/shard_map/all_to_all | solution.py:23
  138.0 1.3 collective-permute-start.2
  139.3 1.8 collective-permute-done.2
  141.1 22.9 %all-to-all-done = bf16[64,1,2,32,128]{4,3,2,1,0:T(8,128)(2,1)} async-done(((bf16[64,1,2,32,128]{4,3,2,1,0:T(8,128)(2,1)}), bf16[64,1,2,32,128]{4,3,2,1,0:T(8,128)(2,1)}, u32[]{:S(2)}, u32[]{:S(2)}) %all-to-all-start) | async-done | bytes 1048608 | tf_op jit(solution)/shard_map/all_to_all | solution.py:23
  165.3 7.9 %all-to-all-start.4 = ((bf16[64,2,32,128]{3,2,1,0:T(8,128)(2,1)}), bf16[64,2,32,128]{3,2,1,0:T(8,128)(2,1)}, u32[]{:S(2)}, u32[]{:S(2)}) async-start(bf16[64,2,32,128]{3,2,1,0:T(8,128)(2,1)} %stack.77), calls=%async_computation.4 | async-start | bytes 2097152 | tf_op jit(solution)/shard_map/all_to_all | solution.py:11
  173.3 8.2 %scatter_custom_fusion = s32[2048]{0:T(1024)S(1)} fusion(s32[2048]{0:T(1024)S(1)} %compare_select_fusion.1, s32[2048]{0:T(1024)S(1)} %iota.3, s32[]{:T(128)} %constant.110.clone.1), kind=kCustom, calls=%fused_computation.99 | custom fusion | bytes 8196 | tf_op jit(solution)/shard_map/scatter | solution.py:91
  181.6 1.3 copy.15
  182.9 9.5 %copy.16 = bf16[2,2048,128]{2,0,1:T(2,128)(2,1)} copy(bf16[2,2048,128]{2,1,0:T(8,128)(2,1)S(1)} %bitcast.179) | data formatting | bytes 2097152 | tf_op jit(solution)/shard_map/squeeze;reshape | solution.py:116
  192.3 15.0 %gather_fusion = bf16[2048,2,128]{2,1,0:T(2,128)(2,1)} fusion(bf16[2,2048,128]{2,0,1:T(2,128)(2,1)} %copy.16, s32[2048]{0:T(1024)S(1)} %fusion.58), kind=kCustom, calls=%fused_computation.clone | custom fusion | bytes 2105344 | tf_op jit(solution)/shard_map/jit(_take)/gather | solution.py:40
  207.4 1.5 select_select_fusion
  210.0 7.1 %gather_fusion.1 = bf16[2048,2,128]{2,1,0:T(2,128)(2,1)S(1)} fusion(bf16[2,2048,128]{2,0,1:T(2,128)(2,1)S(1)} %bitcast.178, s32[2048]{0:T(1024)S(1)} %fusion.58), kind=kCustom, calls=%fused_computation.1.clone | custom fusion | bytes 2105344 | tf_op jit(solution)/shard_map/jit(_take)/gather | solution.py:39
  217.0 7.6 %fusion.14 = (bf16[2,2048,128]{2,0,1:T(2,128)(2,1)S(1)}, bf16[2,2048,128]{2,0,1:T(2,128)(2,1)S(1)}) fusion(bf16[2048,2,128]{2,1,0:T(2,128)(2,1)S(1)} %gather_fusion.1, pred[2048]{0:T(1024)(128)(4,1)S(1)} %compare_and_fusion, bf16[2048,2,128]{2,1,0:T(2,128)(2,1)S(1)} %copy-done.1), kind=kLoop, calls=%fused_computation.42 | loop fusion | flops 1048576 | bytes 4196352 | tf_op jit(solution)/shard_map/jit(_take)/select_n | solution.py:39
  224.6 6.2 %pad_dynamic-slice_fusion = bf16[2,2112,128]{2,0,1:T(2,128)(2,1)S(1)} fusion(s32[]{:T(128)S(6)} %select_n.128, bf16[2,2048,128]{2,0,1:T(2,128)(2,1)S(1)} %get-tuple-element.63), kind=kLoop, calls=%fused_computation.3 | loop fusion | bytes 2129924 | tf_op jit(solution)/shard_map/dynamic_slice | solution.py:42
  231.3 1.7 fusion.68
  234.8 1.3 copy.43
  241.1 3.8 %reshape.404 = f32[32,64,129]{2,1,0:T(8,128)S(1)} reshape(f32[32,8256]{1,0:T(8,128)} %pad.20) | data formatting | bytes 2113536 | tf_op jit(solution)/shard_map/reshape | solution.py:57
  245.2 2.7 %reshape.406 = f32[32,64,129]{2,1,0:T(8,128)S(1)} reshape(f32[32,8256]{1,0:T(8,128)S(1)} %pad.21) | data formatting | bytes 2113536 | tf_op jit(solution)/shard_map/reshape | solution.py:57
  (65 shorter events, 17.0 us)
Async XLA Ops:
  39.8 1.0 copy-start
  41.6 3.1 %collective-permute-start = (bf16[2,32,128]{2,1,0:T(8,128)(2,1)S(1)}, bf16[2,32,128]{2,1,0:T(8,128)(2,1)S(1)}, u32[]{:S(2)}, u32[]{:S(2)}) collective-permute-start(bf16[2,32,128]{2,1,0:T(8,128)(2,1)S(1)} %pad_maximum_fusion.1), channel_id=1, source_target_pairs={{64,0},{128,64},{192,128},{65,1},{129,65},{193,129},{66,2},{130,66... | collective-permute-start | bytes 49160 | tf_op jit(solution)/shard_map/ppermute | solution.py:33
  82.4 43.6 %copy-start.2 = (bf16[1,2,32,128]{3,2,1,0:T(8,128)(2,1)S(1)}, bf16[1,2,32,128]{3,2,1,0:T(8,128)(2,1)}, u32[]{:S(2)}) copy-start(bf16[1,2,32,128]{3,2,1,0:T(8,128)(2,1)} %param.16) | copy-start | bytes 49156
  82.7 4.8 %collective-permute-start.1 = (bf16[2,32,128]{2,1,0:T(8,128)(2,1)S(1)}, bf16[2,32,128]{2,1,0:T(8,128)(2,1)S(1)}, u32[]{:S(2)}, u32[]{:S(2)}) collective-permute-start(bf16[2,32,128]{2,1,0:T(8,128)(2,1)S(1)} %pad_maximum_fusion.2), channel_id=1, source_target_pairs={{64,0},{128,64},{192,128},{65,1},{129,65},{193,129},{66,2},{130,66... | collective-permute-start | bytes 49160 | tf_op jit(solution)/shard_map/ppermute | solution.py:33
  127.3 36.8 %all-to-all-start = ((bf16[64,1,2,32,128]{4,3,2,1,0:T(8,128)(2,1)}), bf16[64,1,2,32,128]{4,3,2,1,0:T(8,128)(2,1)}, u32[]{:S(2)}, u32[]{:S(2)}) async-start(bf16[64,1,2,32,128]{4,3,2,1,0:T(8,128)(2,1)} %broadcast_in_dim.17), calls=%async_computation | async-start | bytes 2097152 | tf_op jit(solution)/shard_map/all_to_all | solution.py:23
  137.8 35.5 %copy-start.3 = (s32[2048]{0:T(1024)S(1)}, s32[2048]{0:T(1024)}, u32[]{:S(2)}) copy-start(s32[2048]{0:T(1024)} %param.17) | copy-start | bytes 24580
  138.0 3.1 %collective-permute-start.2 = (bf16[2,32,128]{2,1,0:T(8,128)(2,1)S(1)}, bf16[2,32,128]{2,1,0:T(8,128)(2,1)S(1)}, u32[]{:S(2)}, u32[]{:S(2)}) collective-permute-start(bf16[2,32,128]{2,1,0:T(8,128)(2,1)S(1)} %pad_maximum_fusion.3), channel_id=1, source_target_pairs={{64,0},{128,64},{192,128},{65,1},{129,65},{193,129},{66,2},{130,66... | collective-permute-start | bytes 49160 | tf_op jit(solution)/shard_map/ppermute | solution.py:33
  165.3 42.0 %all-to-all-start.4 = ((bf16[64,2,32,128]{3,2,1,0:T(8,128)(2,1)}), bf16[64,2,32,128]{3,2,1,0:T(8,128)(2,1)}, u32[]{:S(2)}, u32[]{:S(2)}) async-start(bf16[64,2,32,128]{3,2,1,0:T(8,128)(2,1)} %stack.77), calls=%async_computation.4 | async-start | bytes 2097152 | tf_op jit(solution)/shard_map/all_to_all | solution.py:11
  208.9 8.2 %copy-start.1 = (bf16[2048,2,128]{2,1,0:T(2,128)(2,1)S(1)}, bf16[2048,2,128]{2,1,0:T(2,128)(2,1)}, u32[]{:S(2)}) copy-start(bf16[2048,2,128]{2,1,0:T(2,128)(2,1)} %gather_fusion) | copy-start | bytes 3145732
